TPU v7x, 128 devices: a whole 4x4x4 slice. The times are simulated.
128 devices in a mesh: probe: 4 (over z_hi, core), fsdp: 32 (over y, z_lo, x).
Axes of the slice: x: 4, y: 4, z: 4 (z_hi: 2, z_lo: 2; z = z_hi * 2 + z_lo), core: 2. Of those that a mesh axis runs over, the one named last changes fastest.
Arguments:
- hidden: bfloat16 [65536, 2048], P(('probe', 'fsdp')), may hold values from -6 to 6
- norm_gain: bfloat16 [2048], replicated, may hold values from 0.5 to 1.5
- query_weight: bfloat16 [2048, 2048], P('fsdp'), may hold values from -1 to 1
- key_weight: bfloat16 [2048, 512], P('fsdp'), may hold values from -16 to 16
- value_weight: bfloat16 [2048, 512], P('fsdp'), may hold values from -0.125 to 0.125
- output_weight: bfloat16 [2048, 2048], P('fsdp'), may hold values from -0.125 to 0.125
- probe_seed: int32 [4], P('probe'), may hold values from 0 to 1073741823
Outputs:
- curvature_value: float32 [2048, 512], P('fsdp', 'probe')
- curvature_output: float32 [2048, 2048], P('fsdp', 'probe')
All inputs are finite; a program needn't handle non-finite values.
Results may differ from a plain program's by a relative error of at most 0.024.
Values may be sent and summed in bfloat16 or wider, within the bound.
No kernel may reach another device: no remote copies, remote signals or barrier semaphores. Data moves between devices by JAX's collectives and lax.ppermute only.
A program may use at most 128 MiB of HBM per device.

v0:
```python
import jax
import jax.numpy as jnp
from jax import lax
from jax.sharding import PartitionSpec as P

HEAD_DIM = 128
SEQ = 256
norm_eps = 1e-05
rope_base = 500000.0


def in_one_piece(arrays, axis, dim, along):
    both = jnp.concatenate(arrays, axis=along)
    result, at, finished = (lax.all_gather(both, axis, axis=dim, tiled=True), 0, [])
    for a in arrays:
        finished.append(lax.slice_in_dim(result, at, at + a.shape[along], axis=along))
        at += a.shape[along]
    return tuple(finished)


def split_up(value, dim, size):
    dims = value.shape
    parts = value.reshape(*dims[:dim], size, dims[dim] // size, *dims[dim + 1 :])
    return jnp.moveaxis(parts, dim, 0)


def sent_and_summed(value, axis, dim):
    size = lax.axis_size(axis)
    parts = lax.all_to_all(split_up(value, dim, size), axis, 0, 0, tiled=True)
    return jnp.sum(parts.astype(jnp.float32), axis=0)


def sign_table(seed_value, matrix_code, row_total, column_total):
    row_index = lax.broadcasted_iota(jnp.int32, (row_total, column_total), 0)
    column_index = lax.broadcasted_iota(jnp.int32, (row_total, column_total), 1)
    hashed = (row_index * column_total + column_index) * 747796405 + (
        seed_value * 1664525 + matrix_code * 374761393
    )
    hashed = hashed ^ lax.shift_right_logical(hashed, jnp.int32(15))
    hashed = hashed * 668265261
    hashed = hashed ^ lax.shift_right_logical(hashed, jnp.int32(13))
    hashed = hashed * 1274126177
    hashed = hashed ^ lax.shift_right_logical(hashed, jnp.int32(16))
    return jnp.where(hashed & 1 == 1, 1.0, -1.0).astype(jnp.bfloat16)


def normalize(rows_in, gain_row):
    values = rows_in.astype(jnp.float32)
    inverse = lax.rsqrt(jnp.mean(values * values, axis=1, keepdims=True) + norm_eps)
    return (values * inverse * gain_row.astype(jnp.float32)[None, :]).astype(jnp.bfloat16)


def rotate(projected, head_count):
    row_count = projected.shape[0]
    columns = projected.shape[1]
    head_size = columns // head_count
    half_dim = head_size // 2
    position = (lax.broadcasted_iota(jnp.int32, (row_count, 1), 0) % SEQ).astype(jnp.float32)
    exponent = lax.broadcasted_iota(jnp.int32, (1, half_dim), 1).astype(jnp.float32) * (
        -2.0 / head_size
    )
    frequency = jnp.power(jnp.float32(rope_base), exponent)
    angles = position * frequency
    cosine = jnp.cos(angles)[:, None, :]
    sine_part = jnp.sin(angles)[:, None, :]
    shaped = projected.reshape(row_count, head_count, head_size)
    leading = shaped[:, :, :half_dim]
    trailing = shaped[:, :, half_dim:]
    turned = jnp.concatenate(
        [leading * cosine - trailing * sine_part, trailing * cosine + leading * sine_part], axis=2
    )
    return turned.reshape(row_count, columns).astype(jnp.bfloat16)


def attend(query_rows, key_rows):
    row_count = query_rows.shape[0]
    key_heads = key_rows.shape[1] // HEAD_DIM
    group_size = query_rows.shape[1] // key_rows.shape[1]
    sequences = row_count // SEQ
    grouped_query = query_rows.reshape(sequences, SEQ, key_heads, group_size, HEAD_DIM)
    grouped_key = key_rows.reshape(sequences, SEQ, key_heads, HEAD_DIM)
    scores = jnp.einsum(
        "bqkgd,bskd->bkgqs", grouped_query, grouped_key, preferred_element_type=jnp.float32
    ) * HEAD_DIM ** (-0.5)
    causal_mask = lax.broadcasted_iota(jnp.int32, (SEQ, SEQ), 0) >= lax.broadcasted_iota(
        jnp.int32, (SEQ, SEQ), 1
    )
    scores = jnp.where(causal_mask, scores, -1e30)
    highest = jnp.max(scores, axis=4, keepdims=True)
    raised = jnp.exp(scores - highest)
    return (raised / jnp.sum(raised, axis=4, keepdims=True)).astype(jnp.bfloat16)


def mix_values(attention, value_rows):
    sequences = attention.shape[0]
    key_heads = attention.shape[1]
    group_size = attention.shape[2]
    grouped_value = value_rows.reshape(sequences, SEQ, key_heads, HEAD_DIM)
    combined = jnp.einsum(
        "bkgqs,bskd->bqkgd", attention, grouped_value, preferred_element_type=jnp.float32
    )
    return combined.reshape(sequences * SEQ, key_heads * group_size * HEAD_DIM)


def spread_back(attention, upstream):
    sequences = attention.shape[0]
    key_heads = attention.shape[1]
    group_size = attention.shape[2]
    grouped_upstream = upstream.reshape(sequences, SEQ, key_heads, group_size, HEAD_DIM)
    spread = jnp.einsum(
        "bkgqs,bqkgd->bskd", attention, grouped_upstream, preferred_element_type=jnp.float32
    )
    return spread.reshape(sequences * SEQ, key_heads * HEAD_DIM)


def body(hidden, norm_gain, query_weight, key_weight, value_weight, output_weight, probe_seed):
    seed_value = probe_seed[0]
    normed = normalize(hidden, norm_gain)
    model_width = normed.shape[1]
    query_width = query_weight.shape[1]
    key_width = key_weight.shape[1]
    head_count = query_width // HEAD_DIM
    key_heads = key_width // HEAD_DIM
    contract_rows = (((0,), (0,)), ((), ()))
    contract_columns = (((1,), (1,)), ((), ()))
    portions = in_one_piece((query_weight, key_weight, value_weight), "fsdp", 0, 1)
    query_raw = jnp.dot(normed, portions[0], preferred_element_type=jnp.float32)
    key_raw = jnp.dot(normed, portions[1], preferred_element_type=jnp.float32)
    value_raw = jnp.dot(normed, portions[2], preferred_element_type=jnp.float32)
    query_rows = rotate(query_raw, head_count)
    key_rows = rotate(key_raw, key_heads)
    value_rows = value_raw.astype(jnp.bfloat16)
    attention = attend(query_rows, key_rows)
    context = mix_values(attention, value_rows).astype(jnp.bfloat16)
    signs_value = sign_table(seed_value, 0, model_width, key_width)
    signs_out = sign_table(seed_value, 1, query_width, model_width)
    tangent_value = (
        jnp.dot(normed, signs_value, preferred_element_type=jnp.float32) * model_width ** (-0.5)
    ).astype(jnp.bfloat16)
    tangent_context = mix_values(attention, tangent_value).astype(jnp.bfloat16)
    probe_part = jnp.dot(context, signs_out, preferred_element_type=jnp.float32) * query_width ** (
        -0.5
    )
    whole_out = lax.all_gather(output_weight, "fsdp", axis=0, tiled=True)
    forward_part = jnp.dot(tangent_context, whole_out, preferred_element_type=jnp.float32)
    cotangent = (forward_part + probe_part).astype(jnp.bfloat16)
    back_context = lax.dot_general(
        cotangent, whole_out, contract_columns, preferred_element_type=jnp.float32
    )
    back_value = spread_back(attention, back_context.astype(jnp.bfloat16)).astype(jnp.bfloat16)
    portion = normed
    value_share = sent_and_summed(
        lax.dot_general(
            portion, back_value, contract_rows, preferred_element_type=jnp.float32
        ).astype(jnp.bfloat16),
        "fsdp",
        0,
    )
    portion = context
    output_share = lax.psum_scatter(
        lax.dot_general(
            portion, cotangent, contract_rows, preferred_element_type=jnp.float32
        ).astype(jnp.bfloat16),
        "fsdp",
        scatter_dimension=0,
        tiled=True,
    )
    curvature_value, curvature_output = (
        sent_and_summed(value_share.astype(jnp.bfloat16), "probe", 1),
        sent_and_summed(output_share, "probe", 1),
    )
    return (curvature_value, curvature_output)


def solution(mesh):
    return jax.shard_map(
        body,
        mesh=mesh,
        in_specs=(
            P(("probe", "fsdp"), None),
            P(),
            P("fsdp", None),
            P("fsdp", None),
            P("fsdp", None),
            P("fsdp", None),
            P("probe"),
        ),
        out_specs=(P("fsdp", "probe"), P("fsdp", "probe")),
        check_vma=False,
    )
```

profile of v0, /device:TPU:1, one launch (start us, length us, event | category | flops | bytes accessed | tf_op | source)
XLA Modules:
  0.0 591.7 jit_solution(6584148597963998947)
XLA Ops:
  7.2 0.0 all-gather.3.cloned.1.call-start
  7.2 1.8 pad_maximum_fusion.2
  9.0 0.0 all-gather.3.cloned.1.call-update
  9.0 0.0 all-gather.5.cloned.1.call-start
  9.1 0.7 all-gather.5.cloned.1.call-update
  9.8 0.0 reduce-scatter.2.cloned.1.call-start
  10.5 0.7 convert_element_type.128
  11.2 2.1 fusion.20
  13.3 0.0 copy-start.2
  13.3 4.8 fusion.63
  18.1 1.0 reshape.128
  19.2 1.0 multiply_cosine_fusion
  20.1 148.7 %all-gather.3.cloned.1.call-done = bf16[2048,3072]{1,0:T(8,128)(2,1)} async-done(((bf16[64,3072]{1,0:T(8,128)(2,1)}), bf16[2048,3072]{1,0:T(8,128)(2,1)}) %all-gather.3.cloned.1.call-update) | async-done | bytes 12582928 | tf_op jit(solution)/shard_map/all_gather | solution.py:14
  168.8 0.0 copy-done.2
  168.8 2.9 fusion.57
  171.7 1.0 reshape.131
  172.7 7.5 %fusion.30 = f32[64,8,16,128]{3,1,2,0:T(8,128)S(1)} fusion(bf16[2048,3072]{1,0:T(8,128)(2,1)} %all-gather.3.cloned.1.call-done, bf16[512,2048]{1,0:T(8,128)(2,1)S(1)} %copy-done.2, f32[2048]{0:T(1024)S(1)} %convert_element_type.128, f32[512]{0:T(512)S(1)} %add_rsqrt_fusion), kind=kOutput, calls=%fused_computation.49 | convolution fusion | flops 4299161600 | bytes 14690304 | tf_op jit(solution)/shard_map/dot_general | solution.py:127
  180.2 2.9 copy.83
  183.1 3.0 fusion.36
  186.1 0.1 fusion.102
  186.2 0.3 copy.79
  186.5 0.3 copy.78
  186.8 0.0 copy-start.1
  186.8 0.3 subtract_convert_fusion.1
  187.1 0.3 pad_maximum_fusion.1
  187.4 1.6 copy-done.1
  189.0 1.3 fusion.101
  190.4 2.8 subtract_convert_fusion
  193.2 1.2 pad_maximum_fusion
  194.3 1.3 fusion.40
  195.6 2.5 fusion.103
  198.1 1.1 divide_convert_fusion
  199.3 2.0 copy-done
  201.2 0.0 copy-done.5
  201.2 0.8 convert_bitcast_fusion
  202.0 3.1 copy.59
  205.1 4.5 convert_element_type.143
  209.6 3.0 convert_bitcast_fusion.1
  212.6 3.1 copy.56
  215.7 4.5 convert_element_type.139
  220.2 113.2 %all-gather.5.cloned.1.call-done = bf16[2048,2048]{1,0:T(8,128)(2,1)} async-done(((bf16[64,2048]{1,0:T(8,128)(2,1)}), bf16[2048,2048]{1,0:T(8,128)(2,1)}) %all-gather.5.cloned.1.call-update) | async-done | bytes 8388624 | tf_op jit(solution)/shard_map/all_gather | solution.py:144
  333.4 7.8 %fusion.104 = f32[512,2048]{1,0:T(8,128)S(1)} fusion(bf16[512,2048]{1,0:T(8,128)(2,1)} %convert_element_type.139, bf16[2048,2048]{1,0:T(8,128)(2,1)} %all-gather.5.cloned.1.call-done), kind=kOutput, calls=%fused_computation.127 | convolution fusion | flops 4294967296 | bytes 14680064 | tf_op jit(solution)/shard_map/dot_general | solution.py:145
  341.2 0.0 copy-done.3
  341.2 10.0 %add_convert_fusion = bf16[512,2048]{1,0:T(8,128)(2,1)S(1)} fusion(f32[512,2048]{1,0:T(8,128)S(1)} %fusion.104, bf16[512,2048]{1,0:T(8,128)(2,1)S(1)} %copy-done.3, s32[]{:T(128)S(6)} %add.79, s32[2048]{0:T(1024)S(1)} %iota_multiply_fusion), kind=kOutput, calls=%fused_computation.40 | convolution fusion | flops 4361027584 | bytes 8396804 | tf_op jit(solution)/shard_map/dot_general | solution.py:141
  351.3 1.3 copy-done.6
  352.6 6.8 %convolution_convert_fusion = bf16[2048,2048]{1,0:T(8,128)(2,1)} fusion(bf16[512,2048]{1,0:T(8,128)(2,1)S(1)} %copy-done.3, bf16[512,2048]{1,0:T(8,128)(2,1)S(1)} %add_convert_fusion), kind=kOutput, calls=%fused_computation.26 | convolution fusion | flops 4299161600 | bytes 12582912 | tf_op jit(solution)/shard_map/dot_general | solution.py:161
  359.4 0.0 reduce-scatter.2.cloned.1.call-update
  359.4 1.6 copy-done.7
  360.9 9.4 %convolution_convert_fusion.2 = bf16[512,2048]{1,0:T(8,128)(2,1)} fusion(bf16[512,2048]{1,0:T(8,128)(2,1)S(1)} %copy-done.7, bf16[2048,2048]{1,0:T(8,128)(2,1)} %all-gather.5.cloned.1.call-done), kind=kOutput, calls=%fused_computation.48 | convolution fusion | flops 4296015872 | bytes 12582912 | tf_op jit(solution)/shard_map/dot_general | solution.py:147
  370.3 3.2 reshape.132
  373.5 3.7 fusion.64
  377.3 0.3 copy.62
  377.5 3.0 convolution_convert_fusion.1
  380.6 33.4 %all_to_all.15 = bf16[32,64,512]{2,1,0:T(8,128)(2,1)S(1)} all-to-all(bf16[32,64,512]{2,1,0:T(8,128)(2,1)S(1)} %bitcast.61), channel_id=1, replica_groups=mesh['probe'=4,'fsdp'=32] {'fsdp'}, dimensions={0} | all-to-all | bytes 4194304 | tf_op jit(solution)/shard_map/all_to_all | solution.py:29
  413.9 0.3 reduce_sum.50
  414.3 0.6 copy.63
  414.9 29.9 %all-to-all-start.1 = ((bf16[4,64,128]{2,1,0:T(8,128)(2,1)}), bf16[4,64,128]{2,1,0:T(8,128)(2,1)S(1)}, u32[]{:S(2)}, u32[]{:S(2)}) async-start(bf16[4,64,128]{2,1,0:T(8,128)(2,1)} %copy.63), calls=%async_computation.1 | async-start | bytes 131072 | tf_op jit(solution)/shard_map/all_to_all | solution.py:29
  444.8 102.9 %reduce-scatter.2.cloned.1.call-done = bf16[64,2048]{1,0:T(8,128)(2,1)} async-done(((bf16[2048,2048]{1,0:T(8,128)(2,1)}), bf16[64,2048]{1,0:T(8,128)(2,1)}) %reduce-scatter.2.cloned.1.call-update) | async-done | bytes 262160 | tf_op jit(solution)/shard_map/reduce_scatter | solution.py:160
  547.7 1.7 copy.110
  549.4 0.0 all-to-all-done.1
  549.4 28.3 %all-to-all-start.2 = ((bf16[4,64,512]{2,1,0:T(8,128)(2,1)}), bf16[4,64,512]{2,1,0:T(8,128)(2,1)S(1)}, u32[]{:S(2)}, u32[]{:S(2)}) async-start(bf16[4,64,512]{2,1,0:T(8,128)(2,1)} %bitcast.58), calls=%async_computation.3 | async-start | bytes 524288 | tf_op jit(solution)/shard_map/all_to_all | solution.py:29
  577.7 0.6 convert_reduce_fusion.1
  578.3 5.9 %all-to-all-done.2 = bf16[4,64,512]{2,1,0:T(8,128)(2,1)S(1)} async-done(((bf16[4,64,512]{2,1,0:T(8,128)(2,1)}), bf16[4,64,512]{2,1,0:T(8,128)(2,1)S(1)}, u32[]{:S(2)}, u32[]{:S(2)}) %all-to-all-start.2) | async-done | bytes 262176 | tf_op jit(solution)/shard_map/all_to_all | solution.py:29
  584.2 0.7 convert_reduce_fusion
  (14 shorter events, 0.1 us)
Async XLA Ops:
  7.2 161.7 %all-gather.3.cloned.1.call-start = ((), (), s32[]{:S(2)}) async-start(), calls=%async_computation.4 | async-start | bytes 12976128 | tf_op jit(solution)/shard_map/all_gather | solution.py:14
  9.0 324.4 %all-gather.5.cloned.1.call-start = ((), (), s32[]{:S(2)}) async-start(), calls=%async_computation.5 | async-start | bytes 8650752 | tf_op jit(solution)/shard_map/all_gather | solution.py:144
  9.8 537.9 %reduce-scatter.2.cloned.1.call-start = ((), (), s32[]{:S(2)}) async-start(), calls=%async_computation.6 | async-start | bytes 8650752 | tf_op jit(solution)/shard_map/reduce_scatter | solution.py:160
  13.3 155.6 %copy-start.2 = (bf16[512,2048]{1,0:T(8,128)(2,1)S(1)}, bf16[512,2048]{1,0:T(8,128)(2,1)}, u32[]{:S(2)}) copy-start(bf16[512,2048]{1,0:T(8,128)(2,1)} %param.7) | copy-start | bytes 6291460
  186.8 2.2 copy-start.1
  198.1 3.1 copy-start.5
  199.3 2.0 copy-start
  202.0 7.6 %copy-start.4 = (bf16[2,256,4,128]{3,2,1,0:T(4,128)(2,1)S(1)}, bf16[2,256,4,128]{3,2,1,0:T(4,128)(2,1)}, u32[]{:S(2)}) copy-start(bf16[2,256,4,128]{3,2,1,0:T(4,128)(2,1)} %reshape.128) | copy-start | bytes 1572868
  220.2 121.0 %copy-start.3 = (bf16[512,2048]{1,0:T(8,128)(2,1)S(1)}, bf16[512,2048]{1,0:T(8,128)(2,1)}, u32[]{:S(2)}) copy-start(bf16[512,2048]{1,0:T(8,128)(2,1)} %convert_element_type.143) | copy-start | bytes 6291460
  351.2 1.3 copy-start.6
  359.4 1.6 copy-start.7
  414.9 134.5 %all-to-all-start.1 = ((bf16[4,64,128]{2,1,0:T(8,128)(2,1)}), bf16[4,64,128]{2,1,0:T(8,128)(2,1)S(1)}, u32[]{:S(2)}, u32[]{:S(2)}) async-start(bf16[4,64,128]{2,1,0:T(8,128)(2,1)} %copy.63), calls=%async_computation.1 | async-start | bytes 131072 | tf_op jit(solution)/shard_map/all_to_all | solution.py:29
  549.4 34.8 %all-to-all-start.2 = ((bf16[4,64,512]{2,1,0:T(8,128)(2,1)}), bf16[4,64,512]{2,1,0:T(8,128)(2,1)S(1)}, u32[]{:S(2)}, u32[]{:S(2)}) async-start(bf16[4,64,512]{2,1,0:T(8,128)(2,1)} %bitcast.58), calls=%async_computation.3 | async-start | bytes 524288 | tf_op jit(solution)/shard_map/all_to_all | solution.py:29
Sparse Core Ops, SparseCore 0:
  9.6 159.1 all-gather.2
  170.5 162.9 all-gather.4
  359.5 188.1 reduce-scatter.1
where the time goes:
time: 597 us; the launch traced here: 592 us
  waiting for transfers between devices  371 us (62%)
  matrix products  63.9 us (11%)
  starting transfers between devices  58.3 us (10%)
  local copies, waits for them, and re-layouts  34.3 us (6%)
  blocking collectives  33.4 us (6%)
  other arithmetic  15.4 us (3%)
  between operations  14.9 us (2%)
    all_gather x1, waiting for transfers between devices, in_one_piece(): lax.all_gather(both, axis, axis=dim, tiled=True)  149 us
    all_gather x1, waiting for transfers between devices, body(): whole_out = lax.all_gather(output_weight, 'fsdp', axis=0, tiled=True)  113 us
    reduce_scatter x1, waiting for transfers between devices, body(): lax.psum_scatter(lax.dot_general(portion, cotangent, contract_rows, prefe...  103 us
    all_to_all x2, starting transfers between devices, sent_and_summed(): parts = lax.all_to_all(split_up(value, dim, size), axis, 0, 0, tiled=True)  58.2 us
    all_to_all x1, blocking collectives, sent_and_summed(): parts = lax.all_to_all(split_up(value, dim, size), axis, 0, 0, tiled=True)  33.4 us
  transfers between devices with their start and end apart: 5, of which 4 were waited for; matrix products, arithmetic and copies ran while one was open for 14% of the time, Pallas kernels for 0%

commit v1 on v0

--- a/solution.py
+++ b/solution.py
@@ -7,6 +7,13 @@
 SEQ = 256
 norm_eps = 1e-05
 rope_base = 500000.0
+
+
+def finish_the_joints(frame_in, d0):
+    finding = jnp.stack([frame_in for _ in range(jax.lax.axis_size("fsdp"))])
+    met_up = jax.lax.all_to_all(finding, "fsdp", split_axis=0, concat_axis=0)
+    front = jnp.concatenate(met_up, axis=d0)
+    return front
 
 
 def in_one_piece(arrays, axis, dim, along):
@@ -141,7 +148,7 @@
     probe_part = jnp.dot(context, signs_out, preferred_element_type=jnp.float32) * query_width ** (
         -0.5
     )
-    whole_out = lax.all_gather(output_weight, "fsdp", axis=0, tiled=True)
+    whole_out = finish_the_joints(output_weight, 0)
     forward_part = jnp.dot(tangent_context, whole_out, preferred_element_type=jnp.float32)
     cotangent = (forward_part + probe_part).astype(jnp.bfloat16)
     back_context = lax.dot_general(

time: 597 us -> 580 us (0.972)
  waiting for transfers between devices: 371 us -> 356 us
  blocking collectives: 33.4 us -> 41.2 us
  starting transfers between devices: 58.3 us -> 50.7 us
    all_gather x1 -> x0, waiting for transfers between devices: 113 us -> none  [body(): whole_out = lax.all_gather(output_weight, 'fsdp', axis=0, tiled=True)]
    all_gather x1, waiting for transfers between devices: 149 us -> 246 us  [in_one_piece(): lax.all_gather(both, axis, axis=dim, tiled=True)]
    all_to_all x2, starting transfers between devices: 58.2 us -> 41.1 us  [sent_and_summed(): parts = lax.all_to_all(split_up(value, dim, size), axis, 0, 0, tiled=True)]
    all_to_all x0 -> x1, starting transfers between devices: none -> 9.47 us  [finish_the_joints(): met_up = jax.lax.all_to_all(finding, 'fsdp', split_axis=0, concat_axis=0)]
    all_to_all x1, blocking collectives: 33.4 us -> 41.2 us  [sent_and_summed(): parts = lax.all_to_all(split_up(value, dim, size), axis, 0, 0, tiled=True)]
  transfers between devices with their start and end apart: 5 -> 5, of which waited for: 4 -> 3; matrix products, arithmetic and copies ran while one was open for 14% -> 14% of each run, Pallas kernels for 0% -> 0%
where the time goes in v1:
time: 580 us; the launch traced here: 573 us
  waiting for transfers between devices  356 us (61%)
  matrix products  61.4 us (11%)
  starting transfers between devices  50.7 us (9%)
  blocking collectives  41.2 us (7%)
  local copies, waits for them, and re-layouts  35.4 us (6%)
  between operations  15.2 us (3%)
  other arithmetic  13.1 us (2%)
    all_gather x1, waiting for transfers between devices, in_one_piece(): lax.all_gather(both, axis, axis=dim, tiled=True)  246 us
    reduce_scatter x1, waiting for transfers between devices, body(): lax.psum_scatter(lax.dot_general(portion, cotangent, contract_rows, prefe...  104 us
    all_to_all x1, blocking collectives, sent_and_summed(): parts = lax.all_to_all(split_up(value, dim, size), axis, 0, 0, tiled=True)  41.2 us
    all_to_all x2, starting transfers between devices, sent_and_summed(): parts = lax.all_to_all(split_up(value, dim, size), axis, 0, 0, tiled=True)  41.1 us
  transfers between devices with their start and end apart: 5, of which 3 were waited for; matrix products, arithmetic and copies ran while one was open for 14% of the time, Pallas kernels for 0%

profile of v1, /device:TPU:1, one launch (start us, length us, event | category | flops | bytes accessed | tf_op | source)
XLA Modules:
  0.0 573.4 jit_solution(13524223194545491153)
XLA Ops:
  7.2 0.0 all-gather.2.cloned.1.call-start
  7.2 1.8 pad_maximum_fusion.2
  9.0 0.0 all-gather.2.cloned.1.call-update
  9.0 5.3 stack.2
  14.3 9.5 %all-to-all-start = ((bf16[32,64,2048]{2,1,0:T(8,128)(2,1)}), bf16[32,64,2048]{2,1,0:T(8,128)(2,1)}, u32[]{:S(2)}, u32[]{:S(2)}) async-start(bf16[32,64,2048]{2,1,0:T(8,128)(2,1)} %stack.2), calls=%async_computation | async-start | bytes 16777216 | tf_op jit(solution)/shard_map/all_to_all | solution.py:14
  23.8 0.0 reduce-scatter.2.cloned.1.call-start
  24.5 0.0 copy-done.6
  24.5 0.0 copy-done.2
  24.6 0.5 fusion.20
  25.0 3.1 fusion.63
  28.2 0.9 reshape.133
  29.2 1.0 multiply_cosine_fusion
  30.2 246.3 %all-gather.2.cloned.1.call-done = bf16[2048,3072]{1,0:T(8,128)(2,1)} async-done(((bf16[64,3072]{1,0:T(8,128)(2,1)}), bf16[2048,3072]{1,0:T(8,128)(2,1)}) %all-gather.2.cloned.1.call-update) | async-done | bytes 12582928 | tf_op jit(solution)/shard_map/all_gather | solution.py:21
  276.5 2.9 fusion.57
  279.4 0.9 reshape.137
  280.3 7.1 %fusion.30 = f32[64,8,16,128]{3,1,2,0:T(8,128)S(1)} fusion(bf16[2048,3072]{1,0:T(8,128)(2,1)} %all-gather.2.cloned.1.call-done, bf16[512,2048]{1,0:T(8,128)(2,1)S(1)} %copy-done.2, f32[2048]{0:T(1024)S(1)} %convert_element_type.128, f32[512]{0:T(512)S(1)} %add_rsqrt_fusion), kind=kOutput, calls=%fused_computation.49 | convolution fusion | flops 4299161600 | bytes 14690304 | tf_op jit(solution)/shard_map/dot_general | solution.py:134
  287.4 2.9 copy.83
  290.3 3.0 fusion.36
  293.3 0.1 fusion.102
  293.4 0.3 copy.79
  293.7 0.3 copy.78
  294.0 0.0 copy-start.1
  294.0 0.3 subtract_convert_fusion.1
  294.3 0.3 pad_maximum_fusion.1
  294.6 1.6 copy-done.1
  296.2 1.3 fusion.101
  297.6 2.8 subtract_convert_fusion
  300.4 1.2 pad_maximum_fusion
  301.5 1.3 fusion.40
  302.8 2.6 fusion.103
  305.4 0.0 copy-start.5
  305.4 1.1 divide_convert_fusion
  306.5 0.0 copy-start
  306.5 1.9 copy-done
  308.4 0.0 copy-done.5
  308.4 0.8 convert_bitcast_fusion
  309.2 0.0 copy-start.4
  309.2 3.1 copy.59
  312.3 4.5 convert_element_type.143
  316.8 3.0 convert_bitcast_fusion.1
  319.8 3.1 copy.56
  322.8 3.3 convert_element_type.139
  326.1 0.0 all-to-all-done
  326.2 7.4 %fusion.104 = f32[512,2048]{1,0:T(8,128)S(1)} fusion(bf16[512,2048]{1,0:T(8,128)(2,1)S(1)} %convert_element_type.139, bf16[2048,2048]{1,0:T(8,128)(2,1)} %bitcast.8), kind=kOutput, calls=%fused_computation.127 | convolution fusion | flops 4294967296 | bytes 14680064 | tf_op jit(solution)/shard_map/dot_general | solution.py:152
  333.6 0.0 copy-done.3
  333.6 10.0 %add_convert_fusion = bf16[512,2048]{1,0:T(8,128)(2,1)S(1)} fusion(f32[512,2048]{1,0:T(8,128)S(1)} %fusion.104, bf16[512,2048]{1,0:T(8,128)(2,1)S(1)} %copy-done.3, s32[]{:T(128)S(6)} %add.79, s32[2048]{0:T(1024)S(1)} %iota_multiply_fusion), kind=kOutput, calls=%fused_computation.40 | convolution fusion | flops 4361027584 | bytes 8396804 | tf_op jit(solution)/shard_map/dot_general | solution.py:148
  343.6 6.8 %convolution_convert_fusion = bf16[2048,2048]{1,0:T(8,128)(2,1)} fusion(bf16[512,2048]{1,0:T(8,128)(2,1)S(1)} %copy-done.3, bf16[512,2048]{1,0:T(8,128)(2,1)S(1)} %add_convert_fusion), kind=kOutput, calls=%fused_computation.26 | convolution fusion | flops 4299161600 | bytes 12582912 | tf_op jit(solution)/shard_map/dot_general | solution.py:168
  350.4 0.0 reduce-scatter.2.cloned.1.call-update
  350.5 9.3 %convolution_convert_fusion.2 = bf16[512,2048]{1,0:T(8,128)(2,1)} fusion(bf16[512,2048]{1,0:T(8,128)(2,1)S(1)} %add_convert_fusion, bf16[2048,2048]{1,0:T(8,128)(2,1)} %bitcast.8), kind=kOutput, calls=%fused_computation.48 | convolution fusion | flops 4296015872 | bytes 12582912 | tf_op jit(solution)/shard_map/dot_general | solution.py:154
  359.8 3.2 reshape.138
  363.0 3.7 fusion.64
  366.7 0.3 copy.62
  367.0 3.0 convolution_convert_fusion.1
  370.0 41.2 %all_to_all.20 = bf16[32,64,512]{2,1,0:T(8,128)(2,1)S(1)} all-to-all(bf16[32,64,512]{2,1,0:T(8,128)(2,1)S(1)} %bitcast.62), channel_id=1, replica_groups=mesh['probe'=4,'fsdp'=32] {'fsdp'}, dimensions={0} | all-to-all | bytes 4194304 | tf_op jit(solution)/shard_map/all_to_all | solution.py:36
  411.2 0.3 reduce_sum.50
  411.5 0.6 copy.63
  412.1 14.9 %all-to-all-start.2 = ((bf16[4,64,128]{2,1,0:T(8,128)(2,1)}), bf16[4,64,128]{2,1,0:T(8,128)(2,1)S(1)}, u32[]{:S(2)}, u32[]{:S(2)}) async-start(bf16[4,64,128]{2,1,0:T(8,128)(2,1)} %copy.63), calls=%async_computation.2 | async-start | bytes 131072 | tf_op jit(solution)/shard_map/all_to_all | solution.py:36
  427.1 104.2 %reduce-scatter.2.cloned.1.call-done = bf16[64,2048]{1,0:T(8,128)(2,1)} async-done(((bf16[2048,2048]{1,0:T(8,128)(2,1)}), bf16[64,2048]{1,0:T(8,128)(2,1)}) %reduce-scatter.2.cloned.1.call-update) | async-done | bytes 262160 | tf_op jit(solution)/shard_map/reduce_scatter | solution.py:167
  531.2 1.7 copy.110
  532.9 0.0 all-to-all-done.2
  532.9 26.2 %all-to-all-start.3 = ((bf16[4,64,512]{2,1,0:T(8,128)(2,1)}), bf16[4,64,512]{2,1,0:T(8,128)(2,1)S(1)}, u32[]{:S(2)}, u32[]{:S(2)}) async-start(bf16[4,64,512]{2,1,0:T(8,128)(2,1)} %bitcast.59), calls=%async_computation.4 | async-start | bytes 524288 | tf_op jit(solution)/shard_map/all_to_all | solution.py:36
  559.1 0.6 convert_reduce_fusion.1
  559.8 5.9 %all-to-all-done.3 = bf16[4,64,512]{2,1,0:T(8,128)(2,1)S(1)} async-done(((bf16[4,64,512]{2,1,0:T(8,128)(2,1)}), bf16[4,64,512]{2,1,0:T(8,128)(2,1)S(1)}, u32[]{:S(2)}, u32[]{:S(2)}) %all-to-all-start.3) | async-done | bytes 262176 | tf_op jit(solution)/shard_map/all_to_all | solution.py:36
  565.7 0.7 convert_reduce_fusion
  (12 shorter events, 0.1 us)
Async XLA Ops:
  7.2 269.3 %all-gather.2.cloned.1.call-start = ((), (), s32[]{:S(2)}) async-start(), calls=%async_computation.5 | async-start | bytes 12976128 | tf_op jit(solution)/shard_map/all_gather | solution.py:21
  14.3 10.2 %copy-start.6 = (bf16[2048]{0:T(1024)(128)(2,1)S(1)}, bf16[2048]{0:T(1024)(128)(2,1)}, u32[]{:S(2)}) copy-start(bf16[2048]{0:T(1024)(128)(2,1)} %param.8) | copy-start | bytes 12292
  14.3 10.2 %copy-start.2 = (bf16[512,2048]{1,0:T(8,128)(2,1)S(1)}, bf16[512,2048]{1,0:T(8,128)(2,1)}, u32[]{:S(2)}) copy-start(bf16[512,2048]{1,0:T(8,128)(2,1)} %param.7) | copy-start | bytes 6291460
  14.3 311.8 %all-to-all-start = ((bf16[32,64,2048]{2,1,0:T(8,128)(2,1)}), bf16[32,64,2048]{2,1,0:T(8,128)(2,1)}, u32[]{:S(2)}, u32[]{:S(2)}) async-start(bf16[32,64,2048]{2,1,0:T(8,128)(2,1)} %stack.2), calls=%async_computation | async-start | bytes 16777216 | tf_op jit(solution)/shard_map/all_to_all | solution.py:14
  23.8 507.4 %reduce-scatter.2.cloned.1.call-start = ((), (), s32[]{:S(2)}) async-start(), calls=%async_computation.6 | async-start | bytes 8650752 | tf_op jit(solution)/shard_map/reduce_scatter | solution.py:167
  294.0 2.2 copy-start.1
  305.4 3.1 copy-start.5
  306.5 1.9 copy-start
  309.2 7.5 %copy-start.4 = (bf16[2,256,4,128]{3,2,1,0:T(4,128)(2,1)S(1)}, bf16[2,256,4,128]{3,2,1,0:T(4,128)(2,1)}, u32[]{:S(2)}) copy-start(bf16[2,256,4,128]{3,2,1,0:T(4,128)(2,1)} %reshape.133) | copy-start | bytes 1572868
  326.1 7.5 %copy-start.3 = (bf16[512,2048]{1,0:T(8,128)(2,1)S(1)}, bf16[512,2048]{1,0:T(8,128)(2,1)}, u32[]{:S(2)}) copy-start(bf16[512,2048]{1,0:T(8,128)(2,1)} %convert_element_type.143) | copy-start | bytes 6291460
  412.1 120.8 %all-to-all-start.2 = ((bf16[4,64,128]{2,1,0:T(8,128)(2,1)}), bf16[4,64,128]{2,1,0:T(8,128)(2,1)S(1)}, u32[]{:S(2)}, u32[]{:S(2)}) async-start(bf16[4,64,128]{2,1,0:T(8,128)(2,1)} %copy.63), calls=%async_computation.2 | async-start | bytes 131072 | tf_op jit(solution)/shard_map/all_to_all | solution.py:36
  532.9 32.8 %all-to-all-start.3 = ((bf16[4,64,512]{2,1,0:T(8,128)(2,1)}), bf16[4,64,512]{2,1,0:T(8,128)(2,1)S(1)}, u32[]{:S(2)}, u32[]{:S(2)}) async-start(bf16[4,64,512]{2,1,0:T(8,128)(2,1)} %bitcast.59), calls=%async_computation.4 | async-start | bytes 524288 | tf_op jit(solution)/shard_map/all_to_all | solution.py:36
Sparse Core Ops, SparseCore 0:
  9.6 266.7 all-gather.1
  350.6 180.6 reduce-scatter.1
